TPU v7x, 512 devices: a whole 4x8x8 slice. The times are simulated.
512 devices in a mesh: blk: 128 (over z_lo, y, x), freq: 4 (over z_hi, core).
Axes of the slice: x: 4, y: 8, z: 8 (z_hi: 2, z_lo: 4; z = z_hi * 4 + z_lo), core: 2. Of those that a mesh axis runs over, the one named last changes fastest.
Arguments:
- node_index: int32 [3, 16384], P(None, 'blk'), may hold values from 0 to 63
- emitters: int32 [64], replicated, may hold values from 0 to 16383
- admittance: float32 [2, 16384], P(None, 'blk'), may hold values from -3 to 3
- wavenumbers: float32 [4], P('freq'), may hold values from 20 to 60
Outputs:
- scattered: bfloat16 [4, 2, 64, 16384], P('freq', None, None, 'blk')
- gradient: float32 [16384], P('blk')
All inputs are finite; a program needn't handle non-finite values.
Results may differ from a plain program's by a relative error of at most 0.006.
Values may be sent and summed in bfloat16 or wider, within the bound.
No kernel may reach another device: no remote copies, remote signals or barrier semaphores. Data moves between devices by JAX's collectives and lax.ppermute only.
A program may use at most 64 MiB of HBM per device.

v0:
```python
import jax
import jax.numpy as jnp
from jax import lax
from jax.sharding import Mesh
from jax.sharding import PartitionSpec as P

GRID = 64
BLK = ("blk_0", "blk_1", "blk_2")
soften = 0.0025


def in_order(blocks, dim):
    blocks = jnp.moveaxis(blocks, 0, dim)
    shape = blocks.shape
    return blocks.reshape(*shape[:dim], shape[dim] * shape[dim + 1], *shape[dim + 2 :])


def all_blocks(value, axes, turns):
    blocks = value
    for k in turns:
        blocks = lax.all_gather(blocks, axes[k])
    done = turns[::-1]
    back = [done.index(k) for k in range(len(axes))]
    blocks = blocks.transpose(*back, *range(len(axes), blocks.ndim))
    return blocks.reshape(-1, *value.shape)


def gather_axes(value, axes, turns, dim):
    return in_order(all_blocks(value, axes, turns), dim)


def copy_for_each(value, axis):
    copies = jnp.broadcast_to(value, (lax.axis_size(axis), *value.shape))
    return lax.all_to_all(copies, axis, split_axis=0, concat_axis=0, tiled=True)


def taken_together(value, axis):
    return copy_for_each(value, axis).sum(axis=0)


def green_tile(row_places, col_places, wavenum, strength):
    separation = row_places[:, :, None] - col_places[:, None, :]
    radius = jnp.sqrt(jnp.sum(separation * separation, axis=0) + soften)
    amplitude = strength / radius
    phase_turn = wavenum * radius
    return jnp.stack([amplitude * jnp.cos(phase_turn), amplitude * jnp.sin(phase_turn)]).astype(
        jnp.bfloat16
    )


def apply_tile(tile_data, source):
    real_part = jnp.einsum(
        "tc,rc->tr", source[0], tile_data[0], preferred_element_type=jnp.float32
    ) - jnp.einsum("tc,rc->tr", source[1], tile_data[1], preferred_element_type=jnp.float32)
    imag_part = jnp.einsum(
        "tc,rc->tr", source[1], tile_data[0], preferred_element_type=jnp.float32
    ) + jnp.einsum("tc,rc->tr", source[0], tile_data[1], preferred_element_type=jnp.float32)
    return jnp.stack([real_part, imag_part])


def complex_scale(factor_pair, field_pair):
    factor_real = factor_pair[0][None, :]
    factor_imag = factor_pair[1][None, :]
    real_part = factor_real * field_pair[0] - factor_imag * field_pair[1]
    imag_part = factor_real * field_pair[1] + factor_imag * field_pair[0]
    return jnp.stack([real_part, imag_part])


def row_potential(places, own_places, wavenum, strength, block_count, row_count):
    group_blocks = 1
    for candidate in range(1, block_count + 1):
        if block_count % candidate == 0 and candidate * row_count <= 4096:
            group_blocks = candidate
    group_cols = group_blocks * row_count

    def make_tile(group_id):
        col_places = lax.dynamic_slice_in_dim(places, group_id * group_cols, group_cols, 1)
        return green_tile(own_places, col_places, wavenum, strength)

    tile_stack = lax.map(make_tile, jnp.arange(block_count // group_blocks, dtype=jnp.int32))
    tile_flat = jnp.transpose(tile_stack, (1, 2, 0, 3)).reshape(
        2, row_count, block_count * row_count
    )

    def potential(source, whole_source):
        if whole_source is None:
            whole_source = gather_axes(source, BLK, (0, 1, 2), 2)
        return apply_tile(tile_flat, whole_source)

    return potential


def local(node_index, emitters, admittance, wavenumbers):
    block_count = lax.axis_size(BLK)
    lane_count = lax.axis_size("freq")
    row_count = node_index.shape[1]
    node_count = block_count * row_count
    emitter_count = emitters.shape[0]
    own_block = lax.axis_index(BLK)
    every_index = lax.all_gather(node_index, BLK, axis=1, tiled=True)
    places = every_index.astype(jnp.float32) / GRID
    own_places = node_index.astype(jnp.float32) / GRID
    wavenum = wavenumbers[0]
    strength = float(node_count) ** (-0.5)
    emitter_places = places[:, emitters]
    incident_whole = green_tile(emitter_places, places, wavenum, 1.0)
    incident = lax.dynamic_slice_in_dim(incident_whole, own_block * row_count, row_count, 2)
    potential = row_potential(places, own_places, wavenum, strength, block_count, row_count)
    first_wave = potential(incident, incident_whole)
    weighted = complex_scale(admittance, first_wave).astype(jnp.bfloat16)
    second = potential(weighted, None)
    lane_terms = jnp.sum(first_wave[0] * second[0] - first_wave[1] * second[1], axis=0) / (
        lane_count * emitter_count
    )
    gradient = taken_together(lane_terms, "freq")
    return (second.astype(jnp.bfloat16)[None], gradient)


def solution(mesh):
    split = Mesh(
        mesh.devices.reshape(4, 8, 4, mesh.shape["freq"]), ("blk_0", "blk_1", "blk_2", "freq")
    )
    in_specs = (P(None, BLK), P(), P(None, BLK), P("freq"))
    out_specs = (P("freq", None, None, BLK), P(BLK))
    return jax.shard_map(local, mesh=split, in_specs=in_specs, out_specs=out_specs, check_vma=False)
```

profile of v0, /device:TPU:1, one launch (start us, length us, event | category | flops | bytes accessed | tf_op | source)
XLA Modules:
  0.0 678.0 jit_solution(9046614232390934011)
XLA Ops:
  7.2 0.8 copy.41
  8.7 366.5 %all_gather.19 = s32[3,16384]{0,1:T(8,128)S(1)} all-gather(s32[3,128]{0,1:T(8,128)S(1)} %copy.41), channel_id=1, replica_groups=mesh['blk_0'=4,'blk_1'=8,'blk_2'=4,'freq'=4] {'blk_0','blk_1','blk_2'}, dimensions={1}, use_global_device_ids=true | all-gather | bytes 198144 | tf_op jit(solution)/shard_map/all_gather | solution.py:100
  375.2 3.5 convert_multiply_fusion
  378.8 5.5 copy.43
  384.3 4.0 gather_fusion
  389.0 3.6 multiply_reduce_fusion.1
  392.5 68.6 %while.10 = (s32[]{:T(128)}, bf16[4,2,128,4096]{2,3,0,1:T(8,128)(2,1)}, f32[3,128]{1,0:T(4,128)S(1)}, s32[4]{0:T(128)S(1)}, f32[3,16384]{1,0:T(4,128)S(1)}, /*in...) while((s32[]{:T(128)}, bf16[4,2,128,4096]{2,3,0,1:T(8,128)(2,1)}, f32[3,128]{1,0:T(4,128)S(1)}, ...), condition=%wide.region_3.4_spmd, body=%wide.region_1.3_spmd.sunk | while | flops 8912902 | bytes 19023540 | solution.py:80
  393.8 0.9 multiply_reduce_fusion.3
  394.6 8.9 %fusion.43 = (bf16[1,1,128,4096]{3,2,1,0:T(8,128)(2,1)S(1)}, bf16[1,1,128,4096]{3,2,1,0:T(8,128)(2,1)S(1)}) fusion(f32[]{:T(128)} %get-tuple-element.164, f32[128,4096]{1,0:T(8,128)S(1)} %multiply_reduce_fusion.3), kind=kLoop, calls=%fused_computation.7.clone.1 | loop fusion | flops 3670016 | bytes 4194308 | tf_op jit(solution)/shard_map/while/body/eval_jaxpr/stack | solution.py:46
  403.6 1.5 pad_maximum_fusion.4
  405.1 3.1 copy.77
  408.2 1.4 constant_dynamic-update-slice_fusion.2
  410.9 0.9 multiply_reduce_fusion.3
  411.8 8.9 %fusion.43 = (bf16[1,1,128,4096]{3,2,1,0:T(8,128)(2,1)S(1)}, bf16[1,1,128,4096]{3,2,1,0:T(8,128)(2,1)S(1)}) fusion(f32[]{:T(128)} %get-tuple-element.164, f32[128,4096]{1,0:T(8,128)S(1)} %multiply_reduce_fusion.3), kind=kLoop, calls=%fused_computation.7.clone.1 | loop fusion | flops 3670016 | bytes 4194308 | tf_op jit(solution)/shard_map/while/body/eval_jaxpr/stack | solution.py:46
  420.7 1.5 pad_maximum_fusion.4
  422.2 3.1 copy.77
  425.4 1.5 constant_dynamic-update-slice_fusion.2
  428.1 0.9 multiply_reduce_fusion.3
  428.9 8.9 %fusion.43 = (bf16[1,1,128,4096]{3,2,1,0:T(8,128)(2,1)S(1)}, bf16[1,1,128,4096]{3,2,1,0:T(8,128)(2,1)S(1)}) fusion(f32[]{:T(128)} %get-tuple-element.164, f32[128,4096]{1,0:T(8,128)S(1)} %multiply_reduce_fusion.3), kind=kLoop, calls=%fused_computation.7.clone.1 | loop fusion | flops 3670016 | bytes 4194308 | tf_op jit(solution)/shard_map/while/body/eval_jaxpr/stack | solution.py:46
  437.9 1.5 pad_maximum_fusion.4
  439.4 3.1 copy.77
  442.5 1.5 constant_dynamic-update-slice_fusion.2
  445.2 0.9 multiply_reduce_fusion.3
  446.1 8.9 %fusion.43 = (bf16[1,1,128,4096]{3,2,1,0:T(8,128)(2,1)S(1)}, bf16[1,1,128,4096]{3,2,1,0:T(8,128)(2,1)S(1)}) fusion(f32[]{:T(128)} %get-tuple-element.164, f32[128,4096]{1,0:T(8,128)S(1)} %multiply_reduce_fusion.3), kind=kLoop, calls=%fused_computation.7.clone.1 | loop fusion | flops 3670016 | bytes 4194308 | tf_op jit(solution)/shard_map/while/body/eval_jaxpr/stack | solution.py:46
  455.0 1.5 pad_maximum_fusion.4
  456.6 3.1 copy.77
  459.7 1.5 constant_dynamic-update-slice_fusion.2
  461.2 3.9 fusion.24
  465.1 0.7 copy-done.4
  465.8 16.6 %multiply_convert_fusion.2 = (bf16[64,16384]{1,0:T(8,128)(2,1)S(1)}, bf16[64,16384]{1,0:T(8,128)(2,1)S(1)}) fusion(f32[64,16384]{1,0:T(8,128)S(1)} %copy-done.4, f32[]{:T(128)} %bitcast.66), kind=kLoop, calls=%fused_computation.13 | loop fusion | flops 7340032 | bytes 8388612 | tf_op jit(solution)/shard_map/slice | solution.py:54
  482.5 0.9 fusion.29
  483.3 0.9 fusion.28
  484.2 0.9 convolution_add_fusion
  485.1 0.9 convolution_subtract_fusion
  486.0 11.2 %all_gather.20 = bf16[4,2,64,128]{3,2,1,0:T(8,128)(2,1)} all-gather(bf16[1,2,64,128]{3,2,1,0:T(8,128)(2,1)S(1)} %pad_maximum_fusion.1), channel_id=1, replica_groups=mesh['blk_0'=4,'blk_1'=8,'blk_2'=4,'freq'=4] {'blk_0'}, dimensions={0}, use_global_device_ids=true | all-gather | bytes 163840 | tf_op jit(solution)/shard_map/all_gather | solution.py:21
  497.4 84.1 %all-gather.5.cloned.1.call-done = bf16[32,2,64,128]{3,2,1,0:T(8,128)(2,1)} async-done(((bf16[4,2,64,128]{3,2,1,0:T(8,128)(2,1)}), bf16[32,2,64,128]{3,2,1,0:T(8,128)(2,1)}) %all-gather.5.cloned.1.call-update) | async-done | bytes 1048592 | tf_op jit(solution)/shard_map/all_gather | solution.py:21
  581.6 59.3 %all-gather.7.cloned.1.call-done = bf16[32,4,2,64,128]{4,3,2,1,0:T(8,128)(2,1)} async-done(((bf16[8,4,2,64,128]{4,3,2,1,0:T(8,128)(2,1)}), bf16[32,4,2,64,128]{4,3,2,1,0:T(8,128)(2,1)}) %all-gather.7.cloned.1.call-update) | async-done | bytes 4194320 | tf_op jit(solution)/shard_map/all_gather | solution.py:21
  640.8 3.1 copy.46
  644.0 1.0 fusion.25
  645.0 1.4 copy.48
  646.3 0.8 copy-done.1
  647.2 1.6 fusion.6
  648.8 1.6 fusion.4
  650.4 1.4 copy.47
  651.7 1.6 fusion.16
  653.3 1.5 subtract_reduce_fusion
  655.5 8.2 %all-to-all-start = ((f32[4,1,128]{2,1,0:T(1,128)}), f32[4,1,128]{2,1,0:T(1,128)S(1)}, u32[]{:S(2)}, u32[]{:S(2)}) async-start(f32[4,1,128]{2,1,0:T(1,128)} %broadcast_in_dim.18), calls=%async_computation | async-start | bytes 4096 | tf_op jit(solution)/shard_map/all_to_all | solution.py:34
  664.3 6.4 all-to-all-done
  (37 shorter events, 5.3 us)
Async XLA Ops:
  7.2 574.4 %all-gather.5.cloned.1.call-start = ((), (), s32[]{:S(2)}) async-start(), calls=%async_computation.1 | async-start | bytes 1179648 | tf_op jit(solution)/shard_map/all_gather | solution.py:21
  378.8 5.5 copy-start.6
  461.2 4.7 copy-start.4
  465.1 18.2 %copy-start.2 = (bf16[1,128,4,4096]{1,3,2,0:T(8,128)(2,1)}, bf16[1,128,4,4096]{1,3,2,0:T(8,128)(2,1)S(1)}, u32[]{:S(2)}) copy-start(bf16[1,128,4,4096]{1,3,2,0:T(8,128)(2,1)S(1)} %get-tuple-element.86) | copy-start | bytes 12582916
  465.1 20.0 %copy-start = (bf16[1,128,4,4096]{1,3,2,0:T(8,128)(2,1)}, bf16[1,128,4,4096]{1,3,2,0:T(8,128)(2,1)S(1)}, u32[]{:S(2)}) copy-start(bf16[1,128,4,4096]{1,3,2,0:T(8,128)(2,1)S(1)} %get-tuple-element.85) | copy-start | bytes 12582916
  485.1 0.9 copy-start.5
  497.2 143.6 %all-gather.7.cloned.1.call-start = ((), (), s32[]{:S(2)}) async-start(), calls=%async_computation.2 | async-start | bytes 5242880 | tf_op jit(solution)/shard_map/all_gather | solution.py:21
  645.0 2.2 copy-start.1
  646.3 2.4 copy-start.3
  655.5 15.2 %all-to-all-start = ((f32[4,1,128]{2,1,0:T(1,128)}), f32[4,1,128]{2,1,0:T(1,128)S(1)}, u32[]{:S(2)}, u32[]{:S(2)}) async-start(f32[4,1,128]{2,1,0:T(1,128)} %broadcast_in_dim.18), calls=%async_computation | async-start | bytes 4096 | tf_op jit(solution)/shard_map/all_to_all | solution.py:34
Sparse Core Ops, SparseCore 0:
  497.3 84.1 all-gather.4
  583.6 57.1 all-gather.6
where the time goes:
time: 679 us; the launch traced here: 678 us
  blocking collectives  378 us (56%)
  waiting for transfers between devices  150 us (22%)
  other arithmetic  70.8 us (10%)
  local copies, waits for them, and re-layouts  43.9 us (6%)
  between operations  14.9 us (2%)
  matrix products  9.75 us (1%)
  starting transfers between devices  8.47 us (1%)
    all_gather x1, blocking collectives, local(): every_index = lax.all_gather(node_index, BLK, axis=1, tiled=True)  367 us
    all_gather x2, waiting for transfers between devices, all_blocks(): blocks = lax.all_gather(blocks, axes[k])  143 us
    another operation x8, other arithmetic, green_tile(): jnp.stack([amplitude * jnp.cos(phase_turn), amplitude * jnp.sin(phase_tur...  41.8 us
    dynamic_update_slice x8, local copies, waits for them, and re-layouts, row_potential(): lax.map(make_tile, jnp.arange(block_count // group_blocks, dtype=jnp.int32))  18.3 us
    slice x1, other arithmetic, apply_tile(): source[1]  16.6 us
  transfers between devices with their start and end apart: 3, of which 3 were waited for; matrix products, arithmetic and copies ran while one was open for 0% of the time, Pallas kernels for 0%

commit v1 on v0

--- a/solution.py
+++ b/solution.py
@@ -97,7 +97,7 @@
     node_count = block_count * row_count
     emitter_count = emitters.shape[0]
     own_block = lax.axis_index(BLK)
-    every_index = lax.all_gather(node_index, BLK, axis=1, tiled=True)
+    every_index = jnp.concatenate(lax.all_gather(node_index, BLK), axis=1)
     places = every_index.astype(jnp.float32) / GRID
     own_places = node_index.astype(jnp.float32) / GRID
     wavenum = wavenumbers[0]

time: 679 us -> 632 us (0.931)
  blocking collectives: 378 us -> 326 us
    all_gather x1, blocking collectives: 367 us -> 315 us  [local(): every_index = jnp.concatenate(lax.all_gather(node_index, BLK), axis=1)]
where the time goes in v1:
time: 632 us; the launch traced here: 631 us
  blocking collectives  326 us (52%)
  waiting for transfers between devices  154 us (24%)
  other arithmetic  67.4 us (11%)
  local copies, waits for them, and re-layouts  48 us (8%)
  between operations  14.9 us (2%)
  matrix products  9.75 us (2%)
  starting transfers between devices  8.47 us (1%)
    all_gather x1, blocking collectives, local(): every_index = jnp.concatenate(lax.all_gather(node_index, BLK), axis=1)  315 us
    all_gather x2, waiting for transfers between devices, all_blocks(): blocks = lax.all_gather(blocks, axes[k])  147 us
    another operation x8, other arithmetic, green_tile(): jnp.stack([amplitude * jnp.cos(phase_turn), amplitude * jnp.sin(phase_tur...  41.8 us
    dynamic_update_slice x8, local copies, waits for them, and re-layouts, row_potential(): lax.map(make_tile, jnp.arange(block_count // group_blocks, dtype=jnp.int32))  18.3 us
    slice x1, other arithmetic, apply_tile(): source[1]  16.6 us
  transfers between devices with their start and end apart: 3, of which 3 were waited for; matrix products, arithmetic and copies ran while one was open for 0% of the time, Pallas kernels for 0%

profile of v1, /device:TPU:1, one launch (start us, length us, event | category | flops | bytes accessed | tf_op | source)
XLA Modules:
  0.0 631.0 jit_solution(12522936445613019308)
XLA Ops:
  7.2 0.7 convert_multiply_fusion
  7.9 314.8 %all-gather.3 = s32[128,3,128]{2,1,0:T(4,128)S(1)} all-gather(s32[1,3,128]{2,1,0:T(4,128)} %bitcast.90), channel_id=2, replica_groups=mesh['blk_0'=4,'blk_1'=8,'blk_2'=4,'freq'=4] {'blk_0','blk_1','blk_2'}, dimensions={0}, use_global_device_ids=true | all-gather | bytes 198144 | tf_op jit(solution)/shard_map/all_gather | solution.py:100
  322.8 4.9 copy.41
  327.6 5.5 copy.43
  333.1 4.0 gather_fusion
  337.9 3.6 multiply_reduce_fusion.1
  341.4 68.6 %while.10 = (s32[]{:T(128)}, bf16[4,2,128,4096]{2,3,0,1:T(8,128)(2,1)}, f32[3,128]{1,0:T(4,128)S(1)}, s32[4]{0:T(128)S(1)}, f32[3,16384]{1,0:T(4,128)S(1)}, /*in...) while((s32[]{:T(128)}, bf16[4,2,128,4096]{2,3,0,1:T(8,128)(2,1)}, f32[3,128]{1,0:T(4,128)S(1)}, ...), condition=%wide.region_3.4_spmd, body=%wide.region_1.3_spmd.sunk | while | flops 8912902 | bytes 19023540 | solution.py:80
  342.7 0.9 multiply_reduce_fusion.3
  343.5 8.9 %fusion.43 = (bf16[1,1,128,4096]{3,2,1,0:T(8,128)(2,1)S(1)}, bf16[1,1,128,4096]{3,2,1,0:T(8,128)(2,1)S(1)}) fusion(f32[]{:T(128)} %get-tuple-element.164, f32[128,4096]{1,0:T(8,128)S(1)} %multiply_reduce_fusion.3), kind=kLoop, calls=%fused_computation.7.clone.1 | loop fusion | flops 3670016 | bytes 4194308 | tf_op jit(solution)/shard_map/while/body/eval_jaxpr/stack | solution.py:46
  352.5 1.5 pad_maximum_fusion.4
  354.0 3.1 copy.77
  357.1 1.4 constant_dynamic-update-slice_fusion.2
  359.8 0.9 multiply_reduce_fusion.3
  360.7 8.9 %fusion.43 = (bf16[1,1,128,4096]{3,2,1,0:T(8,128)(2,1)S(1)}, bf16[1,1,128,4096]{3,2,1,0:T(8,128)(2,1)S(1)}) fusion(f32[]{:T(128)} %get-tuple-element.164, f32[128,4096]{1,0:T(8,128)S(1)} %multiply_reduce_fusion.3), kind=kLoop, calls=%fused_computation.7.clone.1 | loop fusion | flops 3670016 | bytes 4194308 | tf_op jit(solution)/shard_map/while/body/eval_jaxpr/stack | solution.py:46
  369.6 1.5 pad_maximum_fusion.4
  371.1 3.1 copy.77
  374.3 1.5 constant_dynamic-update-slice_fusion.2
  377.0 0.9 multiply_reduce_fusion.3
  377.8 8.9 %fusion.43 = (bf16[1,1,128,4096]{3,2,1,0:T(8,128)(2,1)S(1)}, bf16[1,1,128,4096]{3,2,1,0:T(8,128)(2,1)S(1)}) fusion(f32[]{:T(128)} %get-tuple-element.164, f32[128,4096]{1,0:T(8,128)S(1)} %multiply_reduce_fusion.3), kind=kLoop, calls=%fused_computation.7.clone.1 | loop fusion | flops 3670016 | bytes 4194308 | tf_op jit(solution)/shard_map/while/body/eval_jaxpr/stack | solution.py:46
  386.8 1.5 pad_maximum_fusion.4
  388.3 3.1 copy.77
  391.4 1.5 constant_dynamic-update-slice_fusion.2
  394.1 0.9 multiply_reduce_fusion.3
  395.0 8.9 %fusion.43 = (bf16[1,1,128,4096]{3,2,1,0:T(8,128)(2,1)S(1)}, bf16[1,1,128,4096]{3,2,1,0:T(8,128)(2,1)S(1)}) fusion(f32[]{:T(128)} %get-tuple-element.164, f32[128,4096]{1,0:T(8,128)S(1)} %multiply_reduce_fusion.3), kind=kLoop, calls=%fused_computation.7.clone.1 | loop fusion | flops 3670016 | bytes 4194308 | tf_op jit(solution)/shard_map/while/body/eval_jaxpr/stack | solution.py:46
  403.9 1.5 pad_maximum_fusion.4
  405.4 3.1 copy.77
  408.6 1.5 constant_dynamic-update-slice_fusion.2
  410.1 3.9 fusion.24
  414.0 0.7 copy-done.4
  414.7 16.6 %multiply_convert_fusion.2 = (bf16[64,16384]{1,0:T(8,128)(2,1)S(1)}, bf16[64,16384]{1,0:T(8,128)(2,1)S(1)}) fusion(f32[64,16384]{1,0:T(8,128)S(1)} %copy-done.4, f32[]{:T(128)} %bitcast.70), kind=kLoop, calls=%fused_computation.12 | loop fusion | flops 7340032 | bytes 8388612 | tf_op jit(solution)/shard_map/slice | solution.py:54
  431.3 0.9 fusion.29
  432.2 0.9 fusion.28
  433.1 0.9 convolution_add_fusion
  434.0 0.9 convolution_subtract_fusion
  434.9 11.2 %all_gather.24 = bf16[4,2,64,128]{3,2,1,0:T(8,128)(2,1)} all-gather(bf16[1,2,64,128]{3,2,1,0:T(8,128)(2,1)S(1)} %pad_maximum_fusion.1), channel_id=1, replica_groups=mesh['blk_0'=4,'blk_1'=8,'blk_2'=4,'freq'=4] {'blk_0'}, dimensions={0}, use_global_device_ids=true | all-gather | bytes 163840 | tf_op jit(solution)/shard_map/all_gather | solution.py:21
  446.3 88.2 %all-gather.7.cloned.1.call-done = bf16[32,2,64,128]{3,2,1,0:T(8,128)(2,1)} async-done(((bf16[4,2,64,128]{3,2,1,0:T(8,128)(2,1)}), bf16[32,2,64,128]{3,2,1,0:T(8,128)(2,1)}) %all-gather.7.cloned.1.call-update) | async-done | bytes 1048592 | tf_op jit(solution)/shard_map/all_gather | solution.py:21
  534.5 59.3 %all-gather.9.cloned.1.call-done = bf16[32,4,2,64,128]{4,3,2,1,0:T(8,128)(2,1)} async-done(((bf16[8,4,2,64,128]{4,3,2,1,0:T(8,128)(2,1)}), bf16[32,4,2,64,128]{4,3,2,1,0:T(8,128)(2,1)}) %all-gather.9.cloned.1.call-update) | async-done | bytes 4194320 | tf_op jit(solution)/shard_map/all_gather | solution.py:21
  593.8 3.1 copy.46
  596.9 1.0 fusion.25
  597.9 1.4 copy.48
  599.3 0.8 copy-done.1
  600.1 1.6 fusion.6
  601.7 1.6 fusion.4
  603.3 1.4 copy.47
  604.7 1.6 fusion.16
  606.3 1.5 subtract_reduce_fusion
  608.4 8.2 %all-to-all-start = ((f32[4,1,128]{2,1,0:T(1,128)}), f32[4,1,128]{2,1,0:T(1,128)S(1)}, u32[]{:S(2)}, u32[]{:S(2)}) async-start(f32[4,1,128]{2,1,0:T(1,128)} %broadcast_in_dim.18), calls=%async_computation | async-start | bytes 4096 | tf_op jit(solution)/shard_map/all_to_all | solution.py:34
  617.2 6.4 %all-to-all-done = f32[4,1,128]{2,1,0:T(1,128)S(1)} async-done(((f32[4,1,128]{2,1,0:T(1,128)}), f32[4,1,128]{2,1,0:T(1,128)S(1)}, u32[]{:S(2)}, u32[]{:S(2)}) %all-to-all-start) | async-done | bytes 2080 | tf_op jit(solution)/shard_map/all_to_all | solution.py:34
  (37 shorter events, 4.7 us)
Async XLA Ops:
  7.2 527.3 %all-gather.7.cloned.1.call-start = ((), (), s32[]{:S(2)}) async-start(), calls=%async_computation.1 | async-start | bytes 1179648 | tf_op jit(solution)/shard_map/all_gather | solution.py:21
  327.6 5.5 copy-start.6
  410.1 4.7 copy-start.4
  414.0 18.2 %copy-start.2 = (bf16[1,128,4,4096]{1,3,2,0:T(8,128)(2,1)}, bf16[1,128,4,4096]{1,3,2,0:T(8,128)(2,1)S(1)}, u32[]{:S(2)}) copy-start(bf16[1,128,4,4096]{1,3,2,0:T(8,128)(2,1)S(1)} %get-tuple-element.86) | copy-start | bytes 12582916
  414.0 20.0 %copy-start = (bf16[1,128,4,4096]{1,3,2,0:T(8,128)(2,1)}, bf16[1,128,4,4096]{1,3,2,0:T(8,128)(2,1)S(1)}, u32[]{:S(2)}) copy-start(bf16[1,128,4,4096]{1,3,2,0:T(8,128)(2,1)S(1)} %get-tuple-element.85) | copy-start | bytes 12582916
  434.0 0.9 copy-start.5
  446.1 147.7 %all-gather.9.cloned.1.call-start = ((), (), s32[]{:S(2)}) async-start(), calls=%async_computation.2 | async-start | bytes 5242880 | tf_op jit(solution)/shard_map/all_gather | solution.py:21
  597.9 2.2 copy-start.1
  599.3 2.4 copy-start.3
  608.4 15.2 %all-to-all-start = ((f32[4,1,128]{2,1,0:T(1,128)}), f32[4,1,128]{2,1,0:T(1,128)S(1)}, u32[]{:S(2)}, u32[]{:S(2)}) async-start(f32[4,1,128]{2,1,0:T(1,128)} %broadcast_in_dim.18), calls=%async_computation | async-start | bytes 4096 | tf_op jit(solution)/shard_map/all_to_all | solution.py:34
Sparse Core Ops, SparseCore 0:
  446.2 88.2 all-gather.6
  536.6 57.1 all-gather.8
